TPU v7x, 32 devices: a whole 2x2x4 slice. The times are simulated.
32 devices in a mesh: blk: 8 (over y, x, core), heads: 4 (over z).
Axes of the slice: x: 2, y: 2, z: 4, core: 2. Of those that a mesh axis runs over, the one named last changes fastest.
Arguments:
- queries: bfloat16 [2048, 4096], P('blk', 'heads'), may hold values from -5 to 5
- keys: bfloat16 [2048, 1024], P('blk', 'heads'), may hold values from -5 to 5
- values: bfloat16 [2048, 1024], P('blk', 'heads'), may hold values from -6 to 6
- doc_ids: int32 [2048], P('blk'), may hold values from 0 to 7, never falling along the last dimension, each value on 1 to 1024 neighbouring positions
Outputs:
- attended: bfloat16 [2048, 4096], P('blk', 'heads')
Inputs may be any that keep to these rules, and one draw needn't show every extreme that they name: `doc_ids`: Non-decreasing along the sequence; every document has 1024 tokens at most, and some document exactly 1024.
All inputs are finite; a program needn't handle non-finite values.
Results may differ from a plain program's by a relative error of at most 0.0034.
Values may be sent and summed in bfloat16 or wider, within the bound.
A program may use at most 64 MiB of HBM per device.

v0:
```python
import math

import jax
import jax.numpy as jnp
from jax import lax
from jax.sharding import PartitionSpec as P

HEAD_WIDTH = 128
DOC_BLKS = 4


def shifted(value, axis, steps):
    count = lax.axis_size(axis)
    initial, last = (max(0, -steps), min(count, count - steps))
    return lax.ppermute(value, axis, [(source, source + steps) for source in range(initial, last)])


def shards(queries, keys, values, doc_ids):
    row_count = queries.shape[0]
    kv_heads = keys.shape[1] // HEAD_WIDTH
    queries_per_group = queries.shape[1] // keys.shape[1]
    score_scale = 1.0 / math.sqrt(HEAD_WIDTH)
    device_index = lax.axis_index("blk")
    query_heads = queries.reshape(row_count, kv_heads, queries_per_group, HEAD_WIDTH)
    row_numbers = jnp.arange(row_count, dtype=jnp.int32)
    causal = row_numbers[None, :] <= row_numbers[:, None]
    own_block = (keys, values, doc_ids)
    blocks = [(own_block, 0)]
    for offset in range(1, DOC_BLKS + 1):
        blocks.append((shifted((own_block[0], own_block[1], own_block[2]), "blk", offset), offset))
    empty_sum = jnp.zeros((kv_heads, queries_per_group, row_count), jnp.float32)
    empty_num = jnp.zeros((row_count, kv_heads, queries_per_group, HEAD_WIDTH), jnp.float32)
    kept_scores = []
    rowmax = jnp.full((kv_heads, queries_per_group, row_count), -jnp.inf, jnp.float32)
    for received, offset in blocks:
        block_of_keys, block_of_values, key_docs = received
        key_heads = block_of_keys.reshape(row_count, kv_heads, HEAD_WIDTH)
        scores = (
            jnp.einsum("qkgd,skd->kgqs", query_heads, key_heads, preferred_element_type=jnp.float32)
            * score_scale
        )
        allowed = (doc_ids[:, None] == key_docs[None, :]) & (device_index >= offset)
        if offset == 0:
            allowed = allowed & causal
        scores = jnp.where(allowed, scores, -jnp.inf)
        kept_scores.append(scores)
        rowmax = jnp.maximum(rowmax, jnp.max(scores, axis=-1))
    denominator = empty_sum
    numerator = empty_num
    for (received, offset), scores in zip(blocks, kept_scores):
        weights = jnp.exp(scores - rowmax[..., None])
        value_heads = received[1].reshape(row_count, kv_heads, HEAD_WIDTH)
        block_numerator = jnp.einsum(
            "kgqs,skd->qkgd",
            weights.astype(jnp.bfloat16),
            value_heads,
            preferred_element_type=jnp.float32,
        )
        partial_den = jnp.sum(weights, axis=-1)
        denominator = denominator + partial_den
        numerator = numerator + block_numerator
    result = numerator / jnp.transpose(denominator, (2, 0, 1))[..., None]
    return result.reshape(row_count, kv_heads * queries_per_group * HEAD_WIDTH).astype(jnp.bfloat16)


def solution(mesh):
    return jax.shard_map(
        shards,
        mesh=mesh,
        in_specs=(P("blk", "heads"), P("blk", "heads"), P("blk", "heads"), P("blk")),
        out_specs=P("blk", "heads"),
        check_vma=False,
    )
```

profile of v0, /device:TPU:0, one launch (start us, length us, event | category | flops | bytes accessed | tf_op | source)
XLA Modules:
  0.0 64.1 jit_solution(3446450073648893526)
XLA Ops:
  0.0 2.4 %collective-permute-start = (s32[256]{0:T(256)}, s32[256]{0:T(256)S(1)}, u32[]{:S(2)}, u32[]{:S(2)}) collective-permute-start(s32[256]{0:T(256)} %param.7), channel_id=1, source_target_pairs={{0,4},{4,8},{8,12},{12,16},{16,20},{20,24},{24,28},{1,5},{5,9},{9,... | collective-permute-start | bytes 3080 | tf_op jit(solution)/shard_map/ppermute | solution.py:15
  2.4 4.4 %collective-permute-start.2 = (s32[256]{0:T(256)}, s32[256]{0:T(256)S(1)}, u32[]{:S(2)}, u32[]{:S(2)}) collective-permute-start(s32[256]{0:T(256)} %param.7), channel_id=1, source_target_pairs={{0,8},{4,12},{8,16},{12,20},{16,24},{20,28},{1,9},{5,13},{9,17},{1... | collective-permute-start | bytes 3080 | tf_op jit(solution)/shard_map/ppermute | solution.py:15
  6.8 4.3 %collective-permute-start.4 = (s32[256]{0:T(256)}, s32[256]{0:T(256)S(1)}, u32[]{:S(2)}, u32[]{:S(2)}) collective-permute-start(s32[256]{0:T(256)} %param.7), channel_id=1, source_target_pairs={{0,12},{4,16},{8,20},{12,24},{16,28},{1,13},{5,17},{9,21},{13,25},... | collective-permute-start | bytes 3080 | tf_op jit(solution)/shard_map/ppermute | solution.py:15
  11.1 1.3 %collective-permute-start.6 = (s32[256]{0:T(256)}, s32[256]{0:T(256)S(1)}, u32[]{:S(2)}, u32[]{:S(2)}) collective-permute-start(s32[256]{0:T(256)} %param.7), channel_id=1, source_target_pairs={{0,16},{4,20},{8,24},{12,28},{1,17},{5,21},{9,25},{13,29},{2,18},{... | collective-permute-start | bytes 3080 | tf_op jit(solution)/shard_map/ppermute | solution.py:15
  12.4 1.7 %copy.24 = bf16[256,256]{0,1:T(8,128)(2,1)} copy(bf16[256,256]{1,0:T(8,128)(2,1)} %param.5) | data formatting | bytes 262144 | tf_op args[1]
  14.1 1.3 %collective-permute-start.7 = (bf16[256,256]{0,1:T(8,128)(2,1)}, bf16[256,256]{0,1:T(8,128)(2,1)S(1)}, u32[]{:S(2)}, u32[]{:S(2)}) collective-permute-start(bf16[256,256]{0,1:T(8,128)(2,1)} %copy.24), channel_id=1, source_target_pairs={{0,16},{4,20},{8,24},{12,28},{1,17},{5,21},{9,25},{13,29},{2,18},{... | collective-permute-start | bytes 393224 | tf_op jit(solution)/shard_map/ppermute | solution.py:15
  15.4 0.9 %reshape.56 = bf16[256,2,128]{2,1,0:T(2,128)(2,1)S(1)} reshape(bf16[256,256]{1,0:T(8,128)(2,1)} %param.5) | data formatting | bytes 262144 | tf_op jit(solution)/shard_map/reshape | solution.py:37
  16.3 0.0 copy-start.2
  16.4 1.4 %reshape.57 = bf16[256,2,4,128]{3,2,1,0:T(4,128)(2,1)S(1)} reshape(bf16[256,1024]{1,0:T(8,128)(2,1)} %param.4) | data formatting | bytes 1048576 | tf_op jit(solution)/shard_map/reshape | solution.py:24
  17.8 1.0 %copy.72 = bf16[256,256]{0,1:T(8,128)(2,1)S(1)} copy(bf16[256,256]{1,0:T(8,128)(2,1)} %param.6) | data formatting | bytes 262144 | tf_op jit(solution)/shard_map/reshape | solution.py:52
  18.8 0.0 collective-permute-done
  18.8 1.9 %collective-permute-start.5 = (bf16[256,256]{0,1:T(8,128)(2,1)}, bf16[256,256]{0,1:T(8,128)(2,1)S(1)}, u32[]{:S(2)}, u32[]{:S(2)}) collective-permute-start(bf16[256,256]{0,1:T(8,128)(2,1)} %copy.24), channel_id=1, source_target_pairs={{0,12},{4,16},{8,20},{12,24},{16,28},{1,13},{5,17},{9,21},{13,25},... | collective-permute-start | bytes 393224 | tf_op jit(solution)/shard_map/ppermute | solution.py:15
  20.8 0.0 collective-permute-done.2
  20.8 1.6 %collective-permute-start.3 = (bf16[256,256]{0,1:T(8,128)(2,1)}, bf16[256,256]{0,1:T(8,128)(2,1)S(1)}, u32[]{:S(2)}, u32[]{:S(2)}) collective-permute-start(bf16[256,256]{0,1:T(8,128)(2,1)} %copy.24), channel_id=1, source_target_pairs={{0,8},{4,12},{8,16},{12,20},{16,24},{20,28},{1,9},{5,13},{9,17},{1... | collective-permute-start | bytes 393224 | tf_op jit(solution)/shard_map/ppermute | solution.py:15
  22.4 0.0 collective-permute-done.4
  22.4 2.4 %collective-permute-start.1 = (bf16[256,256]{0,1:T(8,128)(2,1)}, bf16[256,256]{0,1:T(8,128)(2,1)S(1)}, u32[]{:S(2)}, u32[]{:S(2)}) collective-permute-start(bf16[256,256]{0,1:T(8,128)(2,1)} %copy.24), channel_id=1, source_target_pairs={{0,4},{4,8},{8,12},{12,16},{16,20},{20,24},{24,28},{1,5},{5,9},{9,... | collective-permute-start | bytes 393224 | tf_op jit(solution)/shard_map/ppermute | solution.py:15
  24.7 0.0 collective-permute-done.6
  24.8 3.1 %collective-permute-start.8 = (bf16[256,256]{1,0:T(8,128)(2,1)}, bf16[256,256]{1,0:T(8,128)(2,1)}, u32[]{:S(2)}, u32[]{:S(2)}) collective-permute-start(bf16[256,256]{1,0:T(8,128)(2,1)} %param.6), channel_id=1, source_target_pairs={{0,4},{4,8},{8,12},{12,16},{16,20},{20,24},{24,28},{1,5},{5,9},{9,... | collective-permute-start | bytes 393224 | tf_op jit(solution)/shard_map/ppermute | solution.py:15
  27.9 1.0 %compare_and_fusion.3 = (pred[256,256]{0,1:T(8,128)(4,1)S(1)}, pred[256,256]{0,1:T(8,128)(4,1)S(1)}, pred[256,256]{0,1:T(8,128)(4,1)S(1)}, pred[256,256]{0,1:T(8,128)(4,1)S(1)}, pred[256,256]{0,1:T(8,128)(4,1)S(1)}) fusion(s32[256]{0:T(256)} %param.7, s32[256]{0:T(256)S(1)} %collective-permute-done, pred[]{:T(512)S(6)} %ge.16, pred[]{:T(512)S(6)} %ge.17, ...), kind=kLoop, calls=%fused_computation.65 | loop fusion | flops 786432 | bytes 332805 | tf_op jit(solution)/shard_map/and | solution.py:42
  28.9 0.5 fusion.63
  29.4 0.0 collective-permute-done.7
  29.4 0.0 copy-done.2
  29.5 2.0 %collective-permute-start.10 = (bf16[256,256]{1,0:T(8,128)(2,1)S(1)}, bf16[256,256]{1,0:T(8,128)(2,1)}, u32[]{:S(2)}, u32[]{:S(2)}) collective-permute-start(bf16[256,256]{1,0:T(8,128)(2,1)S(1)} %copy-done.2), channel_id=1, source_target_pairs={{0,12},{4,16},{8,20},{12,24},{16,28},{1,13},{5,17},{9,21},{13,25},... | collective-permute-start | bytes 393224 | tf_op jit(solution)/shard_map/ppermute | solution.py:15
  31.4 1.9 %fusion.13 = (f32[2,4,256]{2,1,0:T(4,128)S(1)}, f32[2,256,256,4]{2,1,3,0:T(8,128)}) fusion(pred[256,256]{0,1:T(8,128)(4,1)S(1)} %get-tuple-element.13, bf16[256,2,128,1]{0,2,3,1:T(8,128)(2,1)S(1)} %bitcast.120, bf16[256,2,4,128]{3,2,1,0:T(4,128)(2,1)S(1)} %reshape.57), kind=kOutput, calls=%fused_computation.23 | convolution fusion | flops 135788544 | bytes 2826240 | tf_op jit(solution)/shard_map/qkgd,skd->kgqs/dot_general | solution.py:39
  33.3 0.0 collective-permute-done.5
  33.3 1.3 %collective-permute-start.11 = (bf16[256,256]{1,0:T(8,128)(2,1)S(1)}, bf16[256,256]{1,0:T(8,128)(2,1)S(1)}, u32[]{:S(2)}, u32[]{:S(2)}) collective-permute-start(bf16[256,256]{1,0:T(8,128)(2,1)S(1)} %copy-done.2), channel_id=1, source_target_pairs={{0,16},{4,20},{8,24},{12,28},{1,17},{5,21},{9,25},{13,29},{2,18},{... | collective-permute-start | bytes 393224 | tf_op jit(solution)/shard_map/ppermute | solution.py:15
  34.6 1.8 %fusion.12 = (f32[2,4,256]{2,1,0:T(4,128)S(1)}, f32[2,256,256,4]{2,1,3,0:T(8,128)}) fusion(pred[256,256]{0,1:T(8,128)(4,1)S(1)} %get-tuple-element.12, bf16[256,2,128,1]{0,2,3,1:T(8,128)(2,1)S(1)} %bitcast.123, bf16[256,2,4,128]{3,2,1,0:T(4,128)(2,1)S(1)} %reshape.57), kind=kOutput, calls=%fused_computation.22 | convolution fusion | flops 135788544 | bytes 2826240 | tf_op jit(solution)/shard_map/qkgd,skd->kgqs/dot_general | solution.py:39
  36.4 0.0 collective-permute-done.3
  36.4 1.9 %collective-permute-start.9 = (bf16[256,256]{1,0:T(8,128)(2,1)S(1)}, bf16[256,256]{1,0:T(8,128)(2,1)}, u32[]{:S(2)}, u32[]{:S(2)}) collective-permute-start(bf16[256,256]{1,0:T(8,128)(2,1)S(1)} %copy-done.2), channel_id=1, source_target_pairs={{0,8},{4,12},{8,16},{12,20},{16,24},{20,28},{1,9},{5,13},{9,17},{1... | collective-permute-start | bytes 393224 | tf_op jit(solution)/shard_map/ppermute | solution.py:15
  38.4 1.9 %fusion.11 = (f32[2,4,256]{2,1,0:T(4,128)S(1)}, f32[2,256,256,4]{2,1,3,0:T(8,128)}) fusion(pred[256,256]{0,1:T(8,128)(4,1)S(1)} %get-tuple-element.11, bf16[256,2,128,1]{0,2,3,1:T(8,128)(2,1)S(1)} %bitcast.122, bf16[256,2,4,128]{3,2,1,0:T(4,128)(2,1)S(1)} %reshape.57), kind=kOutput, calls=%fused_computation.21 | convolution fusion | flops 135788544 | bytes 2826240 | tf_op jit(solution)/shard_map/qkgd,skd->kgqs/dot_general | solution.py:39
  40.2 0.0 collective-permute-done.1
  40.3 1.9 %fusion.10 = (f32[2,4,256]{2,1,0:T(4,128)S(1)}, f32[2,256,256,4]{2,1,3,0:T(8,128)}) fusion(pred[256,256]{0,1:T(8,128)(4,1)S(1)} %get-tuple-element.10, bf16[256,2,128,1]{0,2,3,1:T(8,128)(2,1)S(1)} %bitcast.121, bf16[256,2,4,128]{3,2,1,0:T(4,128)(2,1)S(1)} %reshape.57), kind=kOutput, calls=%fused_computation.20 | convolution fusion | flops 135788544 | bytes 2826240 | tf_op jit(solution)/shard_map/qkgd,skd->kgqs/dot_general | solution.py:39
  42.1 0.0 collective-permute-done.10
  42.1 1.0 %copy.42 = bf16[256,256]{0,1:T(8,128)(2,1)S(1)} copy(bf16[256,256]{1,0:T(8,128)(2,1)} %collective-permute-done.10) | data formatting | bytes 262144 | tf_op jit(solution)/shard_map/ppermute | solution.py:15
  43.1 3.2 %fusion.21 = f32[2,4,256,128]{2,3,1,0:T(8,128)} fusion(bf16[256,2,128,1]{0,2,3,1:T(8,128)(2,1)S(1)} %bitcast.111, f32[2,256,256,4]{2,1,3,0:T(8,128)} %get-tuple-element.18, f32[2,4,256]{2,1,0:T(4,128)S(1)} %bitcast.114, pred[256,256]{0,1:T(8,128)(4,1)S(1)} %get-tuple-element.12), kind=kOutput, calls=%fused_computation.32 | convolution fusion | flops 136314880 | bytes 3350528 | tf_op jit(solution)/shard_map/kgqs,skd->qkgd/dot_general | solution.py:53
  46.4 0.0 collective-permute-done.11
  46.4 0.1 copy.44
  46.5 0.0 copy-start
  46.5 3.5 %fusion.19 = f32[2,4,256,128]{2,3,1,0:T(8,128)} fusion(bf16[256,2,128,1]{0,2,3,1:T(8,128)(2,1)S(1)} %bitcast.112, f32[2,256,256,4]{2,1,3,0:T(8,128)} %get-tuple-element.16, f32[2,4,256]{2,1,0:T(4,128)S(1)} %bitcast.115, pred[256,256]{0,1:T(8,128)(4,1)S(1)} %get-tuple-element.13), kind=kOutput, calls=%fused_computation.31 | convolution fusion | flops 136314880 | bytes 3350528 | tf_op jit(solution)/shard_map/kgqs,skd->qkgd/dot_general | solution.py:53
  49.9 0.0 copy-done
  49.9 4.6 %fusion.2 = (f32[2,4,256]{2,1,0:T(4,128)S(1)}, f32[2,4,256]{2,1,0:T(4,128)}, f32[2,4,256]{2,1,0:T(4,128)}, f32[2,4,256]{2,1,0:T(4,128)}, f32[2,4,256]{2,1,0:T(4,128)}) fusion(f32[2,256,256,4]{2,1,3,0:T(8,128)} %get-tuple-element.24, f32[2,4,256]{2,1,0:T(4,128)S(1)} %bitcast.116, pred[256,256]{0,1:T(8,128)(4,1)S(1)} %get-tuple-element.10, ...), kind=kLoop, calls=%fused_computation.12 | loop fusion | flops 9426944 | bytes 10797056 | tf_op jit(solution)/shard_map/reduce_sum | solution.py:59
  54.5 0.5 fusion.25
  55.0 0.0 collective-permute-done.8
  55.0 1.0 %copy.38 = bf16[256,256]{0,1:T(8,128)(2,1)S(1)} copy(bf16[256,256]{1,0:T(8,128)(2,1)} %collective-permute-done.8) | data formatting | bytes 262144 | tf_op jit(solution)/shard_map/ppermute | solution.py:15
  56.0 0.0 copy-start.3
  56.1 0.0 copy-start.4
  56.1 0.0 copy-start.5
  56.1 0.0 copy-start.6
  56.1 0.0 copy-start.1
  56.1 3.4 %convolution_add_fusion.1 = f32[2,4,256,128]{2,3,1,0:T(8,128)} fusion(f32[2,4,256,128]{2,3,1,0:T(8,128)S(1)} %fusion.25, bf16[256,2,128,1]{0,2,3,1:T(8,128)(2,1)S(1)} %bitcast.110, f32[2,256,256,4]{2,1,3,0:T(8,128)} %get-tuple-element.24, f32[2,4,256]{2,1,0:T(4,128)S(1)} %bitcast.118, pred[256,256]{0,1:T(8,128)(4,1)S(1)} %get-tuple-element.10), kind=kOutput, calls=%fused_computation.26 | convolution fusion | flops 136577024 | bytes 4399104 | tf_op jit(solution)/shard_map/kgqs,skd->qkgd/dot_general | solution.py:53
  59.5 0.0 copy-done.3
  59.5 0.0 copy-done.4
  59.5 0.0 copy-done.5
  59.5 0.0 copy-done.6
  59.5 0.0 collective-permute-done.9
  59.5 1.0 %copy.40 = bf16[256,256]{0,1:T(8,128)(2,1)S(1)} copy(bf16[256,256]{1,0:T(8,128)(2,1)} %collective-permute-done.9) | data formatting | bytes 262144 | tf_op jit(solution)/shard_map/ppermute | solution.py:15
  60.6 0.0 copy-done.1
  60.6 2.5 %fusion.18 = bf16[256,2,4,128]{0,3,2,1:T(8,128)(2,1)S(1)} fusion(f32[2,4,256,128]{2,3,1,0:T(8,128)} %fusion.19, f32[2,4,256,128]{2,3,1,0:T(8,128)} %fusion.21, f32[2,4,256,128]{2,3,1,0:T(8,128)} %convolution_add_fusion.1, bf16[256,2,128,1]{0,2,3,1:T(8,128)(2,1)S(1)} %bitcast.124, f32[2,256,256,4]{2,1,3,0:T(8,128)S(1)} %copy-done.1, ...), kind=kOutput, calls=%fused_computation.30 | convolution fusion | flops 137625600 | bytes 5980160 | tf_op jit(solution)/shard_map/kgqs,skd->qkgd/dot_general | solution.py:53
  63.1 1.0 %copy.46 = bf16[256,1024]{1,0:T(8,128)(2,1)} copy(bf16[256,1024]{0,1:T(8,128)(2,1)S(1)} %bitcast.113) | data formatting | bytes 1048576 | tf_op jit(solution)/shard_map/convert_element_type | solution.py:63
  (2 shorter events, 0.0 us)
Async XLA Ops:
  0.0 18.8 %collective-permute-start = (s32[256]{0:T(256)}, s32[256]{0:T(256)S(1)}, u32[]{:S(2)}, u32[]{:S(2)}) collective-permute-start(s32[256]{0:T(256)} %param.7), channel_id=1, source_target_pairs={{0,4},{4,8},{8,12},{12,16},{16,20},{20,24},{24,28},{1,5},{5,9},{9,... | collective-permute-start | bytes 3080 | tf_op jit(solution)/shard_map/ppermute | solution.py:15
  2.4 18.4 %collective-permute-start.2 = (s32[256]{0:T(256)}, s32[256]{0:T(256)S(1)}, u32[]{:S(2)}, u32[]{:S(2)}) collective-permute-start(s32[256]{0:T(256)} %param.7), channel_id=1, source_target_pairs={{0,8},{4,12},{8,16},{12,20},{16,24},{20,28},{1,9},{5,13},{9,17},{1... | collective-permute-start | bytes 3080 | tf_op jit(solution)/shard_map/ppermute | solution.py:15
  6.8 15.6 %collective-permute-start.4 = (s32[256]{0:T(256)}, s32[256]{0:T(256)S(1)}, u32[]{:S(2)}, u32[]{:S(2)}) collective-permute-start(s32[256]{0:T(256)} %param.7), channel_id=1, source_target_pairs={{0,12},{4,16},{8,20},{12,24},{16,28},{1,13},{5,17},{9,21},{13,25},... | collective-permute-start | bytes 3080 | tf_op jit(solution)/shard_map/ppermute | solution.py:15
  11.1 13.6 %collective-permute-start.6 = (s32[256]{0:T(256)}, s32[256]{0:T(256)S(1)}, u32[]{:S(2)}, u32[]{:S(2)}) collective-permute-start(s32[256]{0:T(256)} %param.7), channel_id=1, source_target_pairs={{0,16},{4,20},{8,24},{12,28},{1,17},{5,21},{9,25},{13,29},{2,18},{... | collective-permute-start | bytes 3080 | tf_op jit(solution)/shard_map/ppermute | solution.py:15
  14.1 15.3 %collective-permute-start.7 = (bf16[256,256]{0,1:T(8,128)(2,1)}, bf16[256,256]{0,1:T(8,128)(2,1)S(1)}, u32[]{:S(2)}, u32[]{:S(2)}) collective-permute-start(bf16[256,256]{0,1:T(8,128)(2,1)} %copy.24), channel_id=1, source_target_pairs={{0,16},{4,20},{8,24},{12,28},{1,17},{5,21},{9,25},{13,29},{2,18},{... | collective-permute-start | bytes 393224 | tf_op jit(solution)/shard_map/ppermute | solution.py:15
  16.3 13.1 %copy-start.2 = (bf16[256,256]{1,0:T(8,128)(2,1)S(1)}, bf16[256,256]{1,0:T(8,128)(2,1)}, u32[]{:S(2)}) copy-start(bf16[256,256]{1,0:T(8,128)(2,1)} %param.6) | copy-start | bytes 393220
  18.8 14.5 %collective-permute-start.5 = (bf16[256,256]{0,1:T(8,128)(2,1)}, bf16[256,256]{0,1:T(8,128)(2,1)S(1)}, u32[]{:S(2)}, u32[]{:S(2)}) collective-permute-start(bf16[256,256]{0,1:T(8,128)(2,1)} %copy.24), channel_id=1, source_target_pairs={{0,12},{4,16},{8,20},{12,24},{16,28},{1,13},{5,17},{9,21},{13,25},... | collective-permute-start | bytes 393224 | tf_op jit(solution)/shard_map/ppermute | solution.py:15
  20.8 15.7 %collective-permute-start.3 = (bf16[256,256]{0,1:T(8,128)(2,1)}, bf16[256,256]{0,1:T(8,128)(2,1)S(1)}, u32[]{:S(2)}, u32[]{:S(2)}) collective-permute-start(bf16[256,256]{0,1:T(8,128)(2,1)} %copy.24), channel_id=1, source_target_pairs={{0,8},{4,12},{8,16},{12,20},{16,24},{20,28},{1,9},{5,13},{9,17},{1... | collective-permute-start | bytes 393224 | tf_op jit(solution)/shard_map/ppermute | solution.py:15
  22.4 17.9 %collective-permute-start.1 = (bf16[256,256]{0,1:T(8,128)(2,1)}, bf16[256,256]{0,1:T(8,128)(2,1)S(1)}, u32[]{:S(2)}, u32[]{:S(2)}) collective-permute-start(bf16[256,256]{0,1:T(8,128)(2,1)} %copy.24), channel_id=1, source_target_pairs={{0,4},{4,8},{8,12},{12,16},{16,20},{20,24},{24,28},{1,5},{5,9},{9,... | collective-permute-start | bytes 393224 | tf_op jit(solution)/shard_map/ppermute | solution.py:15
  24.8 30.3 %collective-permute-start.8 = (bf16[256,256]{1,0:T(8,128)(2,1)}, bf16[256,256]{1,0:T(8,128)(2,1)}, u32[]{:S(2)}, u32[]{:S(2)}) collective-permute-start(bf16[256,256]{1,0:T(8,128)(2,1)} %param.6), channel_id=1, source_target_pairs={{0,4},{4,8},{8,12},{12,16},{16,20},{20,24},{24,28},{1,5},{5,9},{9,... | collective-permute-start | bytes 393224 | tf_op jit(solution)/shard_map/ppermute | solution.py:15
  29.5 12.7 %collective-permute-start.10 = (bf16[256,256]{1,0:T(8,128)(2,1)S(1)}, bf16[256,256]{1,0:T(8,128)(2,1)}, u32[]{:S(2)}, u32[]{:S(2)}) collective-permute-start(bf16[256,256]{1,0:T(8,128)(2,1)S(1)} %copy-done.2), channel_id=1, source_target_pairs={{0,12},{4,16},{8,20},{12,24},{16,28},{1,13},{5,17},{9,21},{13,25},... | collective-permute-start | bytes 393224 | tf_op jit(solution)/shard_map/ppermute | solution.py:15
  33.3 13.1 %collective-permute-start.11 = (bf16[256,256]{1,0:T(8,128)(2,1)S(1)}, bf16[256,256]{1,0:T(8,128)(2,1)S(1)}, u32[]{:S(2)}, u32[]{:S(2)}) collective-permute-start(bf16[256,256]{1,0:T(8,128)(2,1)S(1)} %copy-done.2), channel_id=1, source_target_pairs={{0,16},{4,20},{8,24},{12,28},{1,17},{5,21},{9,25},{13,29},{2,18},{... | collective-permute-start | bytes 393224 | tf_op jit(solution)/shard_map/ppermute | solution.py:15
  36.4 23.1 %collective-permute-start.9 = (bf16[256,256]{1,0:T(8,128)(2,1)S(1)}, bf16[256,256]{1,0:T(8,128)(2,1)}, u32[]{:S(2)}, u32[]{:S(2)}) collective-permute-start(bf16[256,256]{1,0:T(8,128)(2,1)S(1)} %copy-done.2), channel_id=1, source_target_pairs={{0,8},{4,12},{8,16},{12,20},{16,24},{20,28},{1,9},{5,13},{9,17},{1... | collective-permute-start | bytes 393224 | tf_op jit(solution)/shard_map/ppermute | solution.py:15
  46.5 3.5 %copy-start = (f32[2,256,256,4]{2,1,3,0:T(8,128)S(1)}, f32[2,256,256,4]{2,1,3,0:T(8,128)}, u32[]{:S(2)}) copy-start(f32[2,256,256,4]{2,1,3,0:T(8,128)} %get-tuple-element.16) | copy-start | bytes 6291460
  56.0 3.5 %copy-start.3 = (f32[2,4,256]{2,1,0:T(4,128)S(1)}, f32[2,4,256]{2,1,0:T(4,128)}, u32[]{:S(2)}) copy-start(f32[2,4,256]{2,1,0:T(4,128)} %get-tuple-element.6) | copy-start | bytes 24580
  56.1 3.4 %copy-start.4 = (f32[2,4,256]{2,1,0:T(4,128)S(1)}, f32[2,4,256]{2,1,0:T(4,128)}, u32[]{:S(2)}) copy-start(f32[2,4,256]{2,1,0:T(4,128)} %get-tuple-element.7) | copy-start | bytes 24580
  56.1 3.4 %copy-start.5 = (f32[2,4,256]{2,1,0:T(4,128)S(1)}, f32[2,4,256]{2,1,0:T(4,128)}, u32[]{:S(2)}) copy-start(f32[2,4,256]{2,1,0:T(4,128)} %get-tuple-element.8) | copy-start | bytes 24580
  56.1 3.4 %copy-start.6 = (f32[2,4,256]{2,1,0:T(4,128)S(1)}, f32[2,4,256]{2,1,0:T(4,128)}, u32[]{:S(2)}) copy-start(f32[2,4,256]{2,1,0:T(4,128)} %get-tuple-element.9) | copy-start | bytes 24580
  56.1 4.5 %copy-start.1 = (f32[2,256,256,4]{2,1,3,0:T(8,128)S(1)}, f32[2,256,256,4]{2,1,3,0:T(8,128)}, u32[]{:S(2)}) copy-start(f32[2,256,256,4]{2,1,3,0:T(8,128)} %get-tuple-element.20) | copy-start | bytes 6291460
where the time goes:
time: 64.7 us; the launch traced here: 64.1 us
  starting transfers between devices  27.8 us (43%)
  matrix products  21.1 us (33%)
  local copies, waits for them, and re-layouts  9.19 us (14%)
  other arithmetic  5.65 us (9%)
    ppermute x12, starting transfers between devices, shifted(): lax.ppermute(value, axis, [(source, source + steps) for source in range(i...  27.8 us
    dot_general x5, matrix products, shards(): jnp.einsum('kgqs,skd->qkgd', weights.astype(jnp.bfloat16), value_heads, p...  13.1 us
    dot_general x5, matrix products, shards(): jnp.einsum('qkgd,skd->kgqs', query_heads, key_heads, preferred_element_ty...  7.97 us
    reduce_sum x1, other arithmetic, shards(): partial_den = jnp.sum(weights, axis=-1)  4.59 us
    ppermute x4, local copies, waits for them, and re-layouts, shifted(): lax.ppermute(value, axis, [(source, source + steps) for source in range(i...  3.1 us
    unnamed x15, local copies, waits for them, and re-layouts  1.7 us
    reshape x1, local copies, waits for them, and re-layouts, shards(): queries.reshape(row_count, kv_heads, queries_per_group, HEAD_WIDTH)  1.44 us
  transfers between devices with their start and end apart: 12, of which 0 were waited for; matrix products, arithmetic and copies ran while one was open for 49% of the time, Pallas kernels for 0%

commit v1 on v0

v1 whole, which is shorter than its diff:
```python
import functools
import math

import jax
import jax.numpy as jnp
from jax import lax
from jax.experimental import pallas as pl
from jax.experimental.pallas import tpu as pltpu
from jax.sharding import PartitionSpec as P

HEAD_WIDTH = 128
DOC_BLKS = 4
MESH = pl.DeviceIdType.MESH
NEG = -1e30


def kernel(n, q_hbm, k_hbm, v_hbm, doc_hbm, o_hbm,
           qbuf, kv, docs, qcol, bias, mref, lref, acc, obuf,
           qsem, loadsem, docsem, docsend, docrecv, send, recv, osem):
    rows = q_hbm.shape[0]
    kv_heads = k_hbm.shape[1] // HEAD_WIDTH
    heads = q_hbm.shape[1] // HEAD_WIDTH
    group = heads // kv_heads
    chunks = 2 * kv_heads
    scale = math.log2(math.e) / math.sqrt(HEAD_WIDTH)

    me = lax.axis_index("blk")
    core = lax.rem(me, 2)
    pair = me // 2
    pairs = n // 2

    def load(i):
        src = (k_hbm, v_hbm)[i % 2].at[:, pl.ds((i // 2) * HEAD_WIDTH, HEAD_WIDTH)]
        return pltpu.make_async_copy(src, kv.at[0, i], loadsem.at[i])

    def load_q(h):
        return pltpu.make_async_copy(q_hbm.at[:, pl.ds(h * HEAD_WIDTH, HEAD_WIDTH)], qbuf.at[h], qsem.at[h])

    load_doc = pltpu.make_async_copy(doc_hbm, docs.at[0], docsem)
    for i in range(chunks):
        load(i).start()
    load_doc.start()
    for h in range(heads):
        load_q(h).start()

    barrier = pltpu.get_barrier_semaphore()
    for o in range(1, DOC_BLKS + 1):
        @pl.when(me + o < n)
        def _():
            pl.semaphore_signal(barrier, inc=1, device_id={"blk": me + o}, device_id_type=MESH)

        @pl.when(me >= o)
        def _():
            pl.semaphore_signal(barrier, inc=1, device_id={"blk": me - o}, device_id_type=MESH)
    pl.semaphore_wait(barrier, jnp.minimum(me, DOC_BLKS) + jnp.minimum(n - 1 - me, DOC_BLKS))

    def doc_copy(o):
        return pltpu.make_async_remote_copy(
            src_ref=docs.at[0], dst_ref=docs.at[o], send_sem=docsend.at[o], recv_sem=docrecv.at[o],
            device_id={"blk": me + o}, device_id_type=MESH)

    def copy(src_slot, dst_slot, i, step):
        return pltpu.make_async_remote_copy(
            src_ref=kv.at[src_slot, i], dst_ref=kv.at[dst_slot, i],
            send_sem=send.at[src_slot, dst_slot, i], recv_sem=recv.at[dst_slot, i],
            device_id={"blk": me + step}, device_id_type=MESH)

    far = me + 4 < n
    relayed_source = (lax.rem(pair, 4) == 1) & (pair + 2 < pairs)
    near = (me + 2 < n) & jnp.logical_not(relayed_source)
    relays = lax.rem(pair, 4) == 3
    late = (lax.rem(pair, 4) == 2) & (pair + 1 < pairs)
    has4 = me >= 4
    has2 = me >= 2
    own_flows = [(far, 0, 4, 4), (near, 0, 2, 2), (core == 0, 0, 1, 1)]
    four_flows = [(has4 & relays, 4, 2, -2), (has4 & (core == 1), 4, 3, -1)]
    two_flows = [(has2 & (core == 0), 2, 3, 1), (has2 & (core == 1), 2, 1, -1)]

    def start(flows, i):
        for cond, s, d, step in flows:
            @pl.when(cond)
            def _():
                copy(s, d, i, step).start()

    def arrived(slot, i):
        copy(0, slot, i, slot).wait_recv()

    load_doc.wait()
    for o in range(1, DOC_BLKS + 1):
        @pl.when(me + o < n)
        def _():
            doc_copy(o).start()
    for i in range(chunks):
        load(i).wait()
        start(own_flows, i)

    qcol[...] = jnp.broadcast_to(docs[0, 0:1, :], (HEAD_WIDTH, rows)).T

    def make_bias(o):
        for c in range(rows // HEAD_WIDTH):
            cols = slice(c * HEAD_WIDTH, (c + 1) * HEAD_WIDTH)
            ok = qcol[...] == docs[o, 0:1, cols]
            if o == 0:
                r = lax.broadcasted_iota(jnp.int32, (rows, HEAD_WIDTH), 0)
                s = lax.broadcasted_iota(jnp.int32, (rows, HEAD_WIDTH), 1) + c * HEAD_WIDTH
                ok = ok & (s <= r)
            bias[o, :, cols] = jnp.where(ok, 0.0, NEG)

    def fold(x, op):
        out = x[:, :HEAD_WIDTH]
        for c in range(1, x.shape[1] // HEAD_WIDTH):
            out = op(out, x[:, c * HEAD_WIDTH:(c + 1) * HEAD_WIDTH])
        return out

    def attend(o, g):
        for j in range(group):
            h = g * group + j
            if o == 0:
                load_q(h).wait()
            s = lax.dot_general(qbuf[h], kv[o, 2 * g], (((1,), (1,)), ((), ())),
                                preferred_element_type=jnp.float32)
            s = s + bias[o]
            m = jnp.max(s, axis=-1, keepdims=True)
            if o > 0:
                old = mref[h][:, :1]
                m = jnp.maximum(m, old)
                alpha = jnp.exp2((old - m) * scale)
            w = jnp.exp2((s - m) * scale)
            l = fold(w, jnp.add)
            a = jnp.dot(w.astype(jnp.bfloat16), kv[o, 2 * g + 1], preferred_element_type=jnp.float32)
            if o > 0:
                l = l + lref[h] * alpha
                a = a + acc[h] * alpha
            mref[h] = jnp.broadcast_to(m, (rows, HEAD_WIDTH))
            lref[h] = l
            acc[h] = a

    make_bias(0)
    for g in range(kv_heads):
        attend(0, g)

    for o in range(1, DOC_BLKS + 1):
        @pl.when(me >= o)
        def _():
            doc_copy(o).wait_recv()
            make_bias(o)

    @pl.when(core == 1)
    def _():
        for i in range(chunks):
            arrived(1, i)
        for g in range(kv_heads):
            attend(1, g)

    def take(cond, slot, flows, i):
        @pl.when(cond)
        def _():
            arrived(slot, i)
        start(flows(i), i) if callable(flows) else start(flows, i)

    prompt2 = has2 & jnp.logical_not(late)
    late2 = has2 & late

    def with_cond(cond, flows):
        return [(cond & c, s, d, step) for c, s, d, step in flows]

    for g in range(kv_heads):
        for i in (2 * g, 2 * g + 1):
            take(has4, 4, four_flows, i)
            take(prompt2, 2, with_cond(prompt2, two_flows), i)

        @pl.when(has4)
        def _():
            attend(4, g)

    for g in range(kv_heads):
        for i in (2 * g, 2 * g + 1):
            take(late2, 2, with_cond(late2, two_flows), i)

        @pl.when(has2)
        def _():
            attend(2, g)

    @pl.when(me >= 3)
    def _():
        for g in range(kv_heads):
            for i in (2 * g, 2 * g + 1):
                arrived(3, i)
            attend(3, g)

    @pl.when((core == 0) & (me >= 1))
    def _():
        for g in range(kv_heads):
            for i in (2 * g, 2 * g + 1):
                arrived(1, i)
            attend(1, g)

    def store(h):
        return pltpu.make_async_copy(obuf.at[h], o_hbm.at[:, pl.ds(h * HEAD_WIDTH, HEAD_WIDTH)], osem.at[h])

    for h in range(heads):
        total = jnp.sum(lref[h], axis=-1, keepdims=True)
        obuf[h] = (acc[h] / total).astype(obuf.dtype)
        store(h).start()

    for o in range(1, DOC_BLKS + 1):
        @pl.when(me + o < n)
        def _():
            doc_copy(o).wait_send()
    for cond, s, d, step in own_flows + four_flows + two_flows:
        @pl.when(cond)
        def _():
            for i in range(chunks):
                copy(s, d, i, step).wait_send()
    for h in range(heads):
        store(h).wait()


def shards(n, queries, keys, values, doc_ids):
    rows = queries.shape[0]
    heads = queries.shape[1] // HEAD_WIDTH
    chunks = 2 * (keys.shape[1] // HEAD_WIDTH)
    slots = DOC_BLKS + 1
    any_spec = pl.BlockSpec(memory_space=pl.ANY)
    stat = pltpu.VMEM((heads, rows, HEAD_WIDTH), jnp.float32)
    return pl.pallas_call(
        functools.partial(kernel, n),
        out_shape=jax.ShapeDtypeStruct(queries.shape, jnp.bfloat16),
        in_specs=[any_spec] * 4,
        out_specs=any_spec,
        scratch_shapes=[
            pltpu.VMEM((heads, rows, HEAD_WIDTH), jnp.bfloat16),
            pltpu.VMEM((slots, chunks, rows, HEAD_WIDTH), jnp.bfloat16),
            pltpu.VMEM((slots, 1, rows), jnp.int32),
            pltpu.VMEM((rows, HEAD_WIDTH), jnp.int32),
            pltpu.VMEM((slots, rows, rows), jnp.float32),
            stat, stat, stat,
            pltpu.VMEM((heads, rows, HEAD_WIDTH), jnp.bfloat16),
            pltpu.SemaphoreType.DMA((heads,)),
            pltpu.SemaphoreType.DMA((chunks,)),
            pltpu.SemaphoreType.DMA,
            pltpu.SemaphoreType.DMA((slots,)),
            pltpu.SemaphoreType.DMA((slots,)),
            pltpu.SemaphoreType.DMA((slots, slots, chunks)),
            pltpu.SemaphoreType.DMA((slots, chunks)),
            pltpu.SemaphoreType.DMA((heads,)),
        ],
        compiler_params=pltpu.CompilerParams(collective_id=0, has_side_effects=True),
    )(queries, keys, values, doc_ids.reshape(1, rows))


def solution(mesh):
    return jax.shard_map(
        functools.partial(shards, mesh.shape["blk"]),
        mesh=mesh,
        in_specs=(P("blk", "heads"), P("blk", "heads"), P("blk", "heads"), P("blk")),
        out_specs=P("blk", "heads"),
        check_vma=False,
    )
```

time: 64.7 us -> 27.4 us (0.42)
  the two profiles are of different devices: /device:TPU:0 before, /device:TPU:28 now
where the time goes in v1:
time: 27.4 us; the launch traced here: 27.2 us
  Pallas kernels  25.4 us (93%)
  local copies, waits for them, and re-layouts  1.87 us (7%)
    pallas_call x1, Pallas kernels, shards(): pl.pallas_call(functools.partial(kernel, n), out_shape=jax.ShapeDtypeStru...  25.4 us
    unnamed x1, local copies, waits for them, and re-layouts  1.87 us

profile of v1, /device:TPU:28, one launch (start us, length us, event | category | flops | bytes accessed | tf_op | source)
XLA Modules:
  0.0 27.2 jit_solution(6264624206719810014)
XLA Ops:
  0.0 25.4 %shard_map.46 = bf16[256,1024]{1,0:T(8,128)(2,1)} custom-call(bf16[256,1024]{1,0:T(8,128)(2,1)} %q_hbm.1, bf16[256,256]{1,0:T(8,128)(2,1)} %k_hbm.1, bf16[256,256]{1,0:T(8,128)(2,1)} %v_hbm.1, s32[1,256]{1,0:T(1,128)} %bitcast.1), custom_call_target="tpu_custom_call" | custom-call | tf_op jit(solution)/shard_map/pallas_call | solution.py:226
  25.4 1.9 %copy.6 = bf16[256,1024]{1,0:T(8,128)(2,1)} copy(bf16[256,1024]{1,0:T(8,128)(2,1)} %shard_map.46) | data formatting | bytes 1048576

commit v2 on v1

--- a/solution.py
+++ b/solution.py
@@ -14,9 +14,9 @@
 NEG = -1e30
 
 
-def kernel(n, q_hbm, k_hbm, v_hbm, doc_hbm, o_hbm,
-           qbuf, kv, docs, qcol, bias, mref, lref, acc, obuf,
-           qsem, loadsem, docsem, docsend, docrecv, send, recv, osem):
+def kernel(n, q_hbm, k_hbm, v_hbm, doc_hbm, o_ref,
+           qbuf, kv, docs, bias, mref, lref, acc,
+           qsem, loadsem, docsem, docsend, docrecv, send, recv):
     rows = q_hbm.shape[0]
     kv_heads = k_hbm.shape[1] // HEAD_WIDTH
     heads = q_hbm.shape[1] // HEAD_WIDTH
@@ -83,7 +83,9 @@
                 copy(s, d, i, step).start()
 
     def arrived(slot, i):
-        copy(0, slot, i, slot).wait_recv()
+        pltpu.make_async_remote_copy(
+            src_ref=kv.at[0, i], dst_ref=kv.at[slot, i], send_sem=send.at[0, 1, i], recv_sem=recv.at[slot, i],
+            device_id={"blk": lax.rem(me + 1, n)}, device_id_type=MESH).wait_recv()
 
     load_doc.wait()
     for o in range(1, DOC_BLKS + 1):
@@ -94,50 +96,58 @@
         load(i).wait()
         start(own_flows, i)
 
-    qcol[...] = jnp.broadcast_to(docs[0, 0:1, :], (HEAD_WIDTH, rows)).T
+    def column(row):
+        return jnp.broadcast_to(row, (HEAD_WIDTH, rows)).T
 
     def make_bias(o):
+        key_docs = column(docs[o, 0:1, :])
         for c in range(rows // HEAD_WIDTH):
             cols = slice(c * HEAD_WIDTH, (c + 1) * HEAD_WIDTH)
-            ok = qcol[...] == docs[o, 0:1, cols]
+            ok = key_docs == docs[0, 0:1, cols]
             if o == 0:
-                r = lax.broadcasted_iota(jnp.int32, (rows, HEAD_WIDTH), 0)
-                s = lax.broadcasted_iota(jnp.int32, (rows, HEAD_WIDTH), 1) + c * HEAD_WIDTH
+                s = lax.broadcasted_iota(jnp.int32, (rows, HEAD_WIDTH), 0)
+                r = lax.broadcasted_iota(jnp.int32, (rows, HEAD_WIDTH), 1) + c * HEAD_WIDTH
                 ok = ok & (s <= r)
             bias[o, :, cols] = jnp.where(ok, 0.0, NEG)
 
-    def fold(x, op):
-        out = x[:, :HEAD_WIDTH]
-        for c in range(1, x.shape[1] // HEAD_WIDTH):
-            out = op(out, x[:, c * HEAD_WIDTH:(c + 1) * HEAD_WIDTH])
-        return out
-
-    def attend(o, g):
-        for j in range(group):
-            h = g * group + j
-            if o == 0:
-                load_q(h).wait()
-            s = lax.dot_general(qbuf[h], kv[o, 2 * g], (((1,), (1,)), ((), ())),
-                                preferred_element_type=jnp.float32)
-            s = s + bias[o]
-            m = jnp.max(s, axis=-1, keepdims=True)
-            if o > 0:
-                old = mref[h][:, :1]
-                m = jnp.maximum(m, old)
-                alpha = jnp.exp2((old - m) * scale)
-            w = jnp.exp2((s - m) * scale)
-            l = fold(w, jnp.add)
-            a = jnp.dot(w.astype(jnp.bfloat16), kv[o, 2 * g + 1], preferred_element_type=jnp.float32)
-            if o > 0:
-                l = l + lref[h] * alpha
-                a = a + acc[h] * alpha
-            mref[h] = jnp.broadcast_to(m, (rows, HEAD_WIDTH))
-            lref[h] = l
-            acc[h] = a
+    def own(o):
+        return isinstance(o, int) and o == 0
+
+    def scores(o, h):
+        g = h // group
+        if own(o):
+            load_q(h).wait()
+        s = lax.dot_general(kv[o, 2 * g], qbuf[h], (((1,), (1,)), ((), ())),
+                            preferred_element_type=jnp.float32)
+        s = s + bias[o]
+        return s, jnp.max(s, axis=0, keepdims=True)
+
+    def weigh(o, h, s, m, values_t):
+        if not own(o):
+            old = mref[h]
+            m = jnp.maximum(m, old)
+            alpha = jnp.exp2((old - m) * scale)
+        w = jnp.exp2(s * scale - m * scale)
+        l = jnp.sum(w, axis=0, keepdims=True)
+        a = jnp.dot(values_t, w.astype(jnp.bfloat16), preferred_element_type=jnp.float32)
+        if not own(o):
+            l = l + lref[h] * alpha
+            a = a + acc[h] * alpha
+        mref[h] = m
+        lref[h] = l
+        acc[h] = a
+
+    def attend(o, groups):
+        todo = [h for g in groups for h in range(g * group, (g + 1) * group)]
+        values_t = {g: kv[o, 2 * g + 1].T for g in groups}
+        held = scores(o, todo[0])
+        for k, h in enumerate(todo):
+            ahead = scores(o, todo[k + 1]) if k + 1 < len(todo) else None
+            weigh(o, h, *held, values_t[h // group])
+            held = ahead
 
     make_bias(0)
-    for g in range(kv_heads):
-        attend(0, g)
+    attend(0, range(kv_heads))
 
     for o in range(1, DOC_BLKS + 1):
         @pl.when(me >= o)
@@ -149,8 +159,7 @@
     def _():
         for i in range(chunks):
             arrived(1, i)
-        for g in range(kv_heads):
-            attend(1, g)
+        attend(1, range(kv_heads))
 
     def take(cond, slot, flows, i):
         @pl.when(cond)
@@ -171,37 +180,28 @@
 
         @pl.when(has4)
         def _():
-            attend(4, g)
-
+            attend(4, [g])
+
+        @pl.when(has4 & (core == 0))
+        def _():
+            for i in (2 * g, 2 * g + 1):
+                arrived(3, i)
+            attend(3, [g])
+
+    last = jnp.where(core == 0, 1, 3)
     for g in range(kv_heads):
         for i in (2 * g, 2 * g + 1):
             take(late2, 2, with_cond(late2, two_flows), i)
 
         @pl.when(has2)
         def _():
-            attend(2, g)
-
-    @pl.when(me >= 3)
-    def _():
-        for g in range(kv_heads):
+            attend(2, [g])
             for i in (2 * g, 2 * g + 1):
-                arrived(3, i)
-            attend(3, g)
-
-    @pl.when((core == 0) & (me >= 1))
-    def _():
-        for g in range(kv_heads):
-            for i in (2 * g, 2 * g + 1):
-                arrived(1, i)
-            attend(1, g)
-
-    def store(h):
-        return pltpu.make_async_copy(obuf.at[h], o_hbm.at[:, pl.ds(h * HEAD_WIDTH, HEAD_WIDTH)], osem.at[h])
+                arrived(last, i)
+            attend(last, [g])
 
     for h in range(heads):
-        total = jnp.sum(lref[h], axis=-1, keepdims=True)
-        obuf[h] = (acc[h] / total).astype(obuf.dtype)
-        store(h).start()
+        o_ref[:, h * HEAD_WIDTH:(h + 1) * HEAD_WIDTH] = (acc[h] / lref[h]).T.astype(o_ref.dtype)
 
     for o in range(1, DOC_BLKS + 1):
         @pl.when(me + o < n)
@@ -212,8 +212,6 @@
         def _():
             for i in range(chunks):
                 copy(s, d, i, step).wait_send()
-    for h in range(heads):
-        store(h).wait()
 
 
 def shards(n, queries, keys, values, doc_ids):
@@ -221,21 +219,20 @@
     heads = queries.shape[1] // HEAD_WIDTH
     chunks = 2 * (keys.shape[1] // HEAD_WIDTH)
     slots = DOC_BLKS + 1
-    any_spec = pl.BlockSpec(memory_space=pl.ANY)
-    stat = pltpu.VMEM((heads, rows, HEAD_WIDTH), jnp.float32)
+    hbm_spec = pl.BlockSpec(memory_space=pltpu.HBM)
+    stat = pltpu.VMEM((heads, 1, rows), jnp.float32)
     return pl.pallas_call(
         functools.partial(kernel, n),
-        out_shape=jax.ShapeDtypeStruct(queries.shape, jnp.bfloat16),
-        in_specs=[any_spec] * 4,
-        out_specs=any_spec,
+        out_shape=pltpu.VMEM(queries.shape, jnp.bfloat16),
+        in_specs=[hbm_spec] * 4,
+        out_specs=pl.BlockSpec(memory_space=pltpu.VMEM),
         scratch_shapes=[
             pltpu.VMEM((heads, rows, HEAD_WIDTH), jnp.bfloat16),
             pltpu.VMEM((slots, chunks, rows, HEAD_WIDTH), jnp.bfloat16),
             pltpu.VMEM((slots, 1, rows), jnp.int32),
-            pltpu.VMEM((rows, HEAD_WIDTH), jnp.int32),
             pltpu.VMEM((slots, rows, rows), jnp.float32),
-            stat, stat, stat,
-            pltpu.VMEM((heads, rows, HEAD_WIDTH), jnp.bfloat16),
+            stat, stat,
+            pltpu.VMEM((heads, HEAD_WIDTH, rows), jnp.float32),
             pltpu.SemaphoreType.DMA((heads,)),
             pltpu.SemaphoreType.DMA((chunks,)),
             pltpu.SemaphoreType.DMA,
@@ -243,10 +240,10 @@
             pltpu.SemaphoreType.DMA((slots,)),
             pltpu.SemaphoreType.DMA((slots, slots, chunks)),
             pltpu.SemaphoreType.DMA((slots, chunks)),
-            pltpu.SemaphoreType.DMA((heads,)),
         ],
-        compiler_params=pltpu.CompilerParams(collective_id=0, has_side_effects=True),
-    )(queries, keys, values, doc_ids.reshape(1, rows))
+        compiler_params=pltpu.CompilerParams(collective_id=0, has_side_effects=True,
+                                             vmem_limit_bytes=24 * 2**20),
+    )(*(pltpu.with_memory_space_constraint(x, pltpu.HBM) for x in (queries, keys, values, doc_ids.reshape(1, rows))))
 
 
 def solution(mesh):

time: 27.4 us -> 18.2 us (0.66)
  the two profiles are of different devices: /device:TPU:28 before, /device:TPU:29 now
where the time goes in v2:
time: 18.2 us; the launch traced here: 18 us
  Pallas kernels  17.2 us (95%)
  local copies, waits for them, and re-layouts  0.8 us (4%)
    pallas_call x1, Pallas kernels, shards(): pl.pallas_call(functools.partial(kernel, n), out_shape=pltpu.VMEM(queries...  17.2 us
    unnamed x1, local copies, waits for them, and re-layouts  0.8 us

profile of v2, /device:TPU:29, one launch (start us, length us, event | category | flops | bytes accessed | tf_op | source)
XLA Modules:
  0.0 18.0 jit_solution(14858136853848669486)
XLA Ops:
  0.0 17.2 %shard_map.46 = bf16[256,1024]{1,0:T(8,128)(2,1)S(1)} custom-call(bf16[256,1024]{1,0:T(8,128)(2,1)} %q_hbm.1, bf16[256,256]{1,0:T(8,128)(2,1)} %k_hbm.1, bf16[256,256]{1,0:T(8,128)(2,1)} %v_hbm.1, s32[1,256]{1,0:T(1,128)} %bitcast.1), custom_call_target="tpu_custom_call" | custom-call | tf_op jit(solution)/shard_map/pallas_call | solution.py:224
  17.3 0.8 %copy.6 = bf16[256,1024]{1,0:T(8,128)(2,1)} copy(bf16[256,1024]{1,0:T(8,128)(2,1)S(1)} %shard_map.46) | data formatting | bytes 1048576

commit v3 on v2

--- a/solution.py
+++ b/solution.py
@@ -67,6 +67,7 @@
 
     far = me + 4 < n
     relayed_source = (lax.rem(pair, 4) == 1) & (pair + 2 < pairs)
+    skips = (me + 2 < n) & relayed_source
     near = (me + 2 < n) & jnp.logical_not(relayed_source)
     relays = lax.rem(pair, 4) == 3
     late = (lax.rem(pair, 4) == 2) & (pair + 1 < pairs)
@@ -78,6 +79,8 @@
 
     def start(flows, i):
         for cond, s, d, step in flows:
+            if step == -2 and i == chunks - 1:
+                continue
             @pl.when(cond)
             def _():
                 copy(s, d, i, step).start()
@@ -87,14 +90,15 @@
             src_ref=kv.at[0, i], dst_ref=kv.at[slot, i], send_sem=send.at[0, 1, i], recv_sem=recv.at[slot, i],
             device_id={"blk": lax.rem(me + 1, n)}, device_id_type=MESH).wait_recv()
 
-    load_doc.wait()
-    for o in range(1, DOC_BLKS + 1):
-        @pl.when(me + o < n)
-        def _():
-            doc_copy(o).start()
     for i in range(chunks):
         load(i).wait()
         start(own_flows, i)
+        if i == 0:
+            load_doc.wait()
+            for o in range(1, DOC_BLKS + 1):
+                @pl.when(me + o < n)
+                def _():
+                    doc_copy(o).start()
 
     def column(row):
         return jnp.broadcast_to(row, (HEAD_WIDTH, rows)).T
@@ -149,12 +153,13 @@
     make_bias(0)
     attend(0, range(kv_heads))
 
-    for o in range(1, DOC_BLKS + 1):
+    def receive_docs(o):
         @pl.when(me >= o)
         def _():
             doc_copy(o).wait_recv()
             make_bias(o)
 
+    receive_docs(1)
     @pl.when(core == 1)
     def _():
         for i in range(chunks):
@@ -173,11 +178,19 @@
     def with_cond(cond, flows):
         return [(cond & c, s, d, step) for c, s, d, step in flows]
 
+    for o in range(2, DOC_BLKS + 1):
+        receive_docs(o)
+
     for g in range(kv_heads):
         for i in (2 * g, 2 * g + 1):
             take(has4, 4, four_flows, i)
             take(prompt2, 2, with_cond(prompt2, two_flows), i)
 
+        if g == 0:
+            @pl.when(skips)
+            def _():
+                copy(0, 2, chunks - 1, 2).start()
+
         @pl.when(has4)
         def _():
             attend(4, [g])
@@ -200,6 +213,10 @@
                 arrived(last, i)
             attend(last, [g])
 
+    @pl.when(skips)
+    def _():
+        copy(0, 2, chunks - 1, 2).wait_send()
+
     for h in range(heads):
         o_ref[:, h * HEAD_WIDTH:(h + 1) * HEAD_WIDTH] = (acc[h] / lref[h]).T.astype(o_ref.dtype)
 
@@ -210,7 +227,7 @@
     for cond, s, d, step in own_flows + four_flows + two_flows:
         @pl.when(cond)
         def _():
-            for i in range(chunks):
+            for i in range(chunks - (step == -2)):
                 copy(s, d, i, step).wait_send()
 
 

time: 18.2 us -> 17.8 us (0.978)
  Pallas kernels: 17.2 us -> 16.8 us
    pallas_call x1, Pallas kernels: 17.2 us -> 16.8 us  [shards(): pl.pallas_call(functools.partial(kernel, n), out_shape=pltpu.VMEM(queries...]
where the time goes in v3:
time: 17.8 us; the launch traced here: 17.6 us
  Pallas kernels  16.8 us (94%)
  local copies, waits for them, and re-layouts  0.8 us (4%)
    pallas_call x1, Pallas kernels, shards(): pl.pallas_call(functools.partial(kernel, n), out_shape=pltpu.VMEM(queries...  16.8 us
    unnamed x1, local copies, waits for them, and re-layouts  0.8 us

profile of v3, /device:TPU:29, one launch (start us, length us, event | category | flops | bytes accessed | tf_op | source)
XLA Modules:
  0.0 17.6 jit_solution(11025703021493457592)
XLA Ops:
  0.0 16.8 %shard_map.46 = bf16[256,1024]{1,0:T(8,128)(2,1)S(1)} custom-call(bf16[256,1024]{1,0:T(8,128)(2,1)} %q_hbm.1, bf16[256,256]{1,0:T(8,128)(2,1)} %k_hbm.1, bf16[256,256]{1,0:T(8,128)(2,1)} %v_hbm.1, s32[1,256]{1,0:T(1,128)} %bitcast.1), custom_call_target="tpu_custom_call" | custom-call | tf_op jit(solution)/shard_map/pallas_call | solution.py:241
  16.8 0.8 %copy.6 = bf16[256,1024]{1,0:T(8,128)(2,1)} copy(bf16[256,1024]{1,0:T(8,128)(2,1)S(1)} %shard_map.46) | data formatting | bytes 1048576
